TPU v7x, 512 devices: a whole 4x8x8 slice. The times are simulated.
512 devices in a mesh: owner: 32 (over y, x), rows: 16 (over z, core).
Axes of the slice: x: 4, y: 8, z: 8, core: 2. Of those that a mesh axis runs over, the one named last changes fastest.
Arguments:
- w_down: float32 [64, 1408, 2048], P('owner', None, 'rows'), may hold values from -0.21875 to 0.21875
- router_weight: float32 [2048, 64], P('rows', 'owner'), may hold values from -0.125 to 0.125
- router_gain: float32 [2048], P('rows'), may hold values from 0.25 to 1.75
Outputs:
- serve_down: bfloat16 [64, 1408, 2048], P('owner')
- scale_down: float32 [64, 1408], P('owner')
- serve_router: bfloat16 [2048, 64], replicated
All inputs are finite; a program needn't handle non-finite values. Where the computation divides by a largest or mean magnitude, that divisor is 1e-20 or more.
Results may differ from a plain program's by a relative error of at most 0.001.
Values may be sent and summed in bfloat16 or wider, within the bound.
A program may use at most 128 MiB of HBM per device.

v0:
```python
import jax
import jax.numpy as jnp
from jax import lax
from jax.sharding import PartitionSpec as P


def sent_to_all(x, axis):
    copies = jnp.broadcast_to(x, (lax.axis_size(axis), *x.shape))
    return lax.all_to_all(copies, axis, split_axis=0, concat_axis=0, tiled=True)


def of_everyone(x, axis):
    everything = sent_to_all(x, axis)
    return jnp.max(everything, axis=0)


def laid_out(pieces, dim):
    pieces = jnp.moveaxis(pieces, 0, dim)
    lengths = pieces.shape
    return pieces.reshape(*lengths[:dim], lengths[dim] * lengths[dim + 1], *lengths[dim + 2 :])


def collect(x, axis, dim):
    return laid_out(sent_to_all(x, axis), dim)


def on_device(w_down, router_weight, router_gain):
    scale_down = of_everyone(jnp.max(jnp.abs(w_down), axis=2), "rows")
    narrow_down = (w_down / jnp.expand_dims(scale_down, 2)).astype(jnp.bfloat16)
    serve_down = lax.all_gather(narrow_down, "rows", axis=2, tiled=True)
    part_router = (router_weight * router_gain[:, None]).astype(jnp.bfloat16)
    row_router = lax.all_gather(part_router, "rows", axis=0, tiled=True)
    serve_router = collect(row_router, "owner", 1)
    return (serve_down, scale_down, serve_router)


def solution(mesh):
    placed = (P("owner", None, "rows"), P("rows", "owner"), P("rows"))
    return jax.shard_map(
        on_device,
        mesh=mesh,
        in_specs=placed,
        out_specs=(P("owner", None, None), P("owner", None), P()),
        check_vma=False,
    )
```

profile of v0, /device:TPU:1, one launch (start us, length us, event | category | flops | bytes accessed | tf_op | source)
XLA Modules:
  0.0 126.5 jit_solution(15650277266331991324)
XLA Ops:
  7.2 0.0 copy-start
  7.2 0.0 all-gather.2.cloned.1.call-start
  7.2 1.9 %abs_reduce_fusion = f32[2,1408]{1,0:T(2,128)S(1)} fusion(f32[2,1408,128]{2,1,0:T(8,128)} %param.3), kind=kLoop, calls=%fused_computation.1 | loop fusion | flops 718080 | bytes 1453056 | tf_op jit(solution)/shard_map/reduce_max | solution.py:28
  9.2 21.2 %all_to_all.10 = f32[16,2,1408]{2,1,0:T(2,128)S(1)} all-to-all(f32[16,2,1408]{2,1,0:T(2,128)S(1)} %broadcast_in_dim.8), channel_id=1, replica_groups=mesh['owner'=32,'rows'=16] {'rows'}, dimensions={0} | all-to-all | bytes 360448 | tf_op jit(solution)/shard_map/all_to_all | solution.py:9
  30.4 0.1 reduce_max.19
  30.5 0.0 copy-done
  30.5 0.0 copy-start.1
  30.5 0.0 copy-start.2
  30.5 0.0 copy-start.3
  30.5 1.3 %divide_convert_fusion = bf16[2,1408,128]{2,1,0:T(8,128)(2,1)} fusion(f32[2,1408,128]{2,1,0:T(8,128)S(1)} %copy-done, f32[2,1408]{1,0:T(2,128)S(1)} %reduce_max.19), kind=kLoop, calls=%fused_computation | loop fusion | flops 720896 | bytes 2173952 | tf_op jit(solution)/shard_map/convert_element_type | solution.py:29
  31.8 0.0 all-gather.2.cloned.1.call-update
  31.9 0.0 copy-done.1
  31.9 0.0 copy-done.2
  31.9 0.0 copy-done.3
  31.9 14.6 %all_gather.7 = bf16[2048,2]{0,1:T(2,128)(2,1)S(1)} all-gather(bf16[128,2]{0,1:T(2,128)(2,1)S(1)} %multiply_convert_fusion), channel_id=1, replica_groups=mesh['owner'=32,'rows'=16] {'rows'}, dimensions={0}, use_global_device_ids=true | all-gather | bytes 8704 | tf_op jit(solution)/shard_map/all_gather | solution.py:32
  46.5 0.1 broadcast_in_dim.9
  46.7 21.1 %all_to_all.11 = bf16[32,2048,2]{1,2,0:T(2,128)(2,1)S(1)} all-to-all(bf16[32,2048,2]{1,2,0:T(2,128)(2,1)S(1)} %broadcast_in_dim.9), channel_id=1, replica_groups=mesh['owner'=32,'rows'=16] {'owner'}, dimensions={0} | all-to-all | bytes 524288 | tf_op jit(solution)/shard_map/all_to_all | solution.py:9
  67.8 0.8 reshape.11
  68.6 40.9 %all-gather.2.cloned.1.call-done = bf16[2,1408,2048]{2,1,0:T(8,128)(2,1)} async-done(((bf16[2,1408,128]{2,1,0:T(8,128)(2,1)}), bf16[2,1408,2048]{2,1,0:T(8,128)(2,1)}) %all-gather.2.cloned.1.call-update) | async-done | bytes 11534352 | tf_op jit(solution)/shard_map/all_gather | solution.py:30
  109.5 10.1 %copy.9 = bf16[2,1408,2048]{2,1,0:T(8,128)(2,1)} copy(bf16[2,1408,2048]{2,1,0:T(8,128)(2,1)} %all-gather.2.cloned.1.call-done) | data formatting | bytes 23068672
  (2 shorter events, 0.1 us)
Async XLA Ops:
  7.2 23.3 %copy-start = (f32[2,1408,128]{2,1,0:T(8,128)S(1)}, f32[2,1408,128]{2,1,0:T(8,128)}, u32[]{:S(2)}) copy-start(f32[2,1408,128]{2,1,0:T(8,128)} %param.3) | copy-start | bytes 4325380
  7.2 102.4 %all-gather.2.cloned.1.call-start = ((), (), s32[]{:S(2)}) async-start(), calls=%async_computation.2 | async-start | bytes 12255232 | tf_op jit(solution)/shard_map/all_gather | solution.py:30
  30.5 1.4 %copy-start.1 = (f32[2,1408]{1,0:T(2,128)}, f32[2,1408]{1,0:T(2,128)S(1)}, u32[]{:S(2)}) copy-start(f32[2,1408]{1,0:T(2,128)S(1)} %reduce_max.19) | copy-start | bytes 33796
  30.5 1.4 %copy-start.2 = (f32[128,2]{0,1:T(2,128)S(1)}, f32[128,2]{0,1:T(2,128)}, u32[]{:S(2)}) copy-start(f32[128,2]{0,1:T(2,128)} %param.4) | copy-start | bytes 3076
  30.5 1.4 %copy-start.3 = (f32[128]{0:T(128)S(1)}, f32[128]{0:T(128)}, u32[]{:S(2)}) copy-start(f32[128]{0:T(128)} %param.5) | copy-start | bytes 1540
Sparse Core Ops, SparseCore 0:
  32.0 77.4 all-gather.1
where the time goes:
time: 127 us; the launch traced here: 126 us
  blocking collectives  57 us (45%)
  waiting for transfers between devices  41 us (32%)
  between operations  14.1 us (11%)
  local copies, waits for them, and re-layouts  11.1 us (9%)
  other arithmetic  3.29 us (3%)
    all_to_all x2, blocking collectives, sent_to_all(): return lax.all_to_all(copies, axis, split_axis=0, concat_axis=0, tiled=True)  42.3 us
    all_gather x1, waiting for transfers between devices, on_device(): serve_down = lax.all_gather(narrow_down, 'rows', axis=2, tiled=True)  40.9 us
    all_gather x1, blocking collectives, on_device(): row_router = lax.all_gather(part_router, 'rows', axis=0, tiled=True)  14.6 us
    unnamed x9, local copies, waits for them, and re-layouts  10.1 us
  transfers between devices with their start and end apart: 1, of which 1 were waited for; matrix products, arithmetic and copies ran while one was open for 1% of the time, Pallas kernels for 0%

commit v1 on v0

v1 whole, which is shorter than its diff:
```python
import functools

import jax
import jax.numpy as jnp
from jax import lax
from jax.experimental import pallas as pl
from jax.experimental.pallas import tpu as pltpu
from jax.sharding import PartitionSpec as P

MESH = pl.DeviceIdType.MESH
BF16 = jnp.bfloat16
F32 = jnp.float32

E = 2
ROWS = 1408
LANES = 128
Z = 8
NR = 16
X, Y = 4, 8
BLOCKS = ROWS // LANES
KE = 4
K = E * KE
CH = ROWS // KE
HALF = K // 2
STEPS = 3 * K + HALF


def kernel(w_hbm, rw_hbm, gain_hbm, out, scale_out, router_out,
           w, rw, gain, mx, inv, rb,
           in_sem, mx_send, mx_recv, ring_send, right_recv, left_recv,
           die_send, die_recv, own_recv,
           r1_send, r1_recv, rx_send, rx_recv, ry_send, ry_recv):
    owner = lax.axis_index("owner")
    rows = lax.axis_index("rows")
    z, core = rows // 2, rows % 2
    x, y = owner % X, owner // X
    barrier = pltpu.get_barrier_semaphore()

    def at_rows(r):
        return {"rows": r}

    column = [(rows + d) % NR for d in range(1, NR)]
    across_x = [y * X + (x + d) % X for d in range(1, X)]
    across_y = [((y + d) % Y) * X + x for d in range(1, Y)]
    right = ((z + 1) % Z) * 2 + core
    left = ((z + Z - 1) % Z) * 2 + core
    partner = z * 2 + 1 - core

    loads = [pltpu.make_async_copy(w_hbm.at[e], w.at[e], in_sem.at[e]) for e in range(E)]
    loads.append(pltpu.make_async_copy(rw_hbm, rw, in_sem.at[E]))
    loads.append(pltpu.make_async_copy(gain_hbm, gain, in_sem.at[E + 1]))
    for load in loads:
        load.start()
    for r in column:
        pl.semaphore_signal(barrier, inc=1, device_id=at_rows(r), device_id_type=MESH)
    for o in across_x + across_y:
        pl.semaphore_signal(barrier, inc=1, device_id={"owner": o}, device_id_type=MESH)

    def maxima(e):
        loads[e].wait()
        for b in range(BLOCKS):
            block = jnp.abs(w[e, b * LANES:(b + 1) * LANES, :])
            mx[rows, e, b:b + 1, :] = jnp.max(block.T, axis=0, keepdims=True)

    def mx_copies(e):
        return [
            pltpu.make_async_remote_copy(
                src_ref=mx.at[rows, e], dst_ref=mx.at[rows, e],
                send_sem=mx_send.at[e, i], recv_sem=mx_recv.at[e, rows],
                device_id=at_rows(r), device_id_type=MESH)
            for i, r in enumerate(column)
        ]

    maxima(0)
    pl.semaphore_wait(barrier, len(column) + len(across_x) + len(across_y))
    sent = [mx_copies(e) for e in range(E)]
    for copy in sent[0]:
        copy.start()
    r1 = [
        pltpu.make_async_remote_copy(
            src_ref=rb.at[owner, rows], dst_ref=rb.at[owner, rows],
            send_sem=r1_send.at[i], recv_sem=r1_recv.at[rows],
            device_id=at_rows(r), device_id_type=MESH)
        for i, r in enumerate(column)
    ]
    maxima(1)
    for copy in sent[1]:
        copy.start()
    loads[E].wait()
    loads[E + 1].wait()
    rb[owner, rows] = (rw[...] * gain[...]).astype(BF16)
    for copy in r1:
        copy.start()

    def mx_wait(e):
        for r in column:
            pltpu.make_async_copy(mx.at[r, e], mx.at[r, e], mx_recv.at[e, r]).wait()

    def cells(origin, k):
        e, part = k // KE, k % KE
        first = pl.multiple_of(part * CH, CH)
        lanes = pl.multiple_of(origin * LANES, LANES)
        return out.at[e, pl.ds(first, CH), pl.ds(lanes, LANES)]

    def ring(to, origin, k, send, recv):
        part = cells(origin, k)
        return pltpu.make_async_remote_copy(
            src_ref=part, dst_ref=part, send_sem=send, recv_sem=recv,
            device_id=at_rows(to), device_id_type=MESH)

    def die(origin, k, send, recv):
        return ring(partner, origin, k, send, recv)

    for e in range(E):
        mx_wait(e)
        scale = jnp.max(mx[:, e], axis=0)
        inv[e] = 1.0 / scale
        for b in range(BLOCKS):
            scale_out[e:e + 1, b * LANES:(b + 1) * LANES] = scale[b:b + 1]
        done = 0
        for part in range(KE):
            need = -(-(part + 1) * CH // LANES)
            for b in range(done, need):
                factor = jnp.broadcast_to(inv[e, b:b + 1, :], (LANES, LANES)).T
                block = w[e, b * LANES:(b + 1) * LANES, :] * factor
                out[e, b * LANES:(b + 1) * LANES, pl.ds(pl.multiple_of(rows * LANES, LANES), LANES)] = block.astype(BF16)
            done = need
            k = e * KE + part
            ring(right, rows, k, ring_send.at[0, k], right_recv.at[k]).start()
            ring(left, rows, k, ring_send.at[1, k], left_recv.at[k]).start()
            die(rows, k, die_send.at[0, k], own_recv.at[k]).start()

    def step(j, _):
        d, k = j // K, j % K
        for side, (to, recv, sign) in enumerate(((right, right_recv, Z - 1), (left, left_recv, 1))):
            origin = ((z + sign * (d + 1)) % Z) * 2 + core
            far = k if side == 0 else HALF + k
            kk = jnp.where(d == 3, far, k)
            part = ring(to, origin, kk, ring_send.at[side, j], recv.at[j])
            part.wait_recv()

            @pl.when(d < 2)
            def _():
                ring(to, origin, k, ring_send.at[side, K + j], recv.at[K + j]).start()

            far_here = k - side * HALF

            @pl.when((d == 2) & (far_here >= 0) & (far_here < HALF))
            def _():
                ring(to, origin, k, ring_send.at[side, 3 * K + far_here], recv.at[3 * K + far_here]).start()

            die(origin, kk, die_send.at[1 + side, j], die_recv.at[side, j]).start()
        return 0

    def run(a, b):
        lax.fori_loop(a, b, step, 0)

    run(0, K)
    for r in column:
        pltpu.make_async_copy(rb.at[owner, r], rb.at[owner, r], r1_recv.at[r]).wait()
    rx = [
        pltpu.make_async_remote_copy(
            src_ref=rb.at[owner], dst_ref=rb.at[owner],
            send_sem=rx_send.at[i], recv_sem=rx_recv.at[x],
            device_id={"owner": o}, device_id_type=MESH)
        for i, o in enumerate(across_x)
    ]
    for copy in rx:
        copy.start()
    run(K, K + HALF)
    for i, o in enumerate(across_x):
        pltpu.make_async_copy(rb.at[o], rb.at[o], rx_recv.at[o % X]).wait()
    mine = rb.at[pl.ds(y * X, X)]
    ry = [
        pltpu.make_async_remote_copy(
            src_ref=mine, dst_ref=mine,
            send_sem=ry_send.at[i], recv_sem=ry_recv.at[y],
            device_id={"owner": o}, device_id_type=MESH)
        for i, o in enumerate(across_y)
    ]
    for copy in ry:
        copy.start()
    run(K + HALF, 2 * K)
    for o in across_y:
        theirs = rb.at[pl.ds((o // X) * X, X)]
        pltpu.make_async_copy(theirs, theirs, ry_recv.at[o // X]).wait()
    for o in range(X * Y):
        for r in range(NR):
            router_out[2 * o:2 * o + 2, r * LANES:(r + 1) * LANES] = rb[o, r]
    run(2 * K, STEPS)

    for k in range(K):
        die(partner, k, die_send.at[0, k], own_recv.at[k]).wait_recv()
        die(rows, k, die_send.at[0, k], own_recv.at[k]).wait_send()

    def last(j, _):
        d, k = j // K, j % K
        for side, sign in enumerate((Z - 1, 1)):
            theirs = ((z + sign * (d + 1)) % Z) * 2 + 1 - core
            kk = jnp.where(d == 3, HALF * side + k, k)
            there = die(theirs, kk, die_send.at[1 + side, j], die_recv.at[side, j])
            there.wait_recv()
            there.wait_send()
            ring(right, theirs, kk, ring_send.at[side, j], right_recv.at[j]).wait_send()
        return 0

    lax.fori_loop(0, STEPS, last, 0)
    for e in range(E):
        for copy in sent[e]:
            copy.wait_send()
    for copy in r1 + rx + ry:
        copy.wait_send()


def on_device(w_down, router_weight, router_gain):
    dma = pltpu.SemaphoreType.DMA
    out, scale, router = pl.pallas_call(
        kernel,
        name="serve",
        out_shape=(
            jax.ShapeDtypeStruct((E, ROWS, NR * LANES), BF16),
            jax.ShapeDtypeStruct((E, ROWS), F32),
            jax.ShapeDtypeStruct((E * X * Y, NR * LANES), BF16),
        ),
        in_specs=[pl.BlockSpec(memory_space=pltpu.HBM)] * 3,
        out_specs=(
            pl.BlockSpec(memory_space=pltpu.VMEM),
            pl.BlockSpec(memory_space=pltpu.VMEM),
            pl.BlockSpec(memory_space=pltpu.VMEM),
        ),
        scratch_shapes=[
            pltpu.VMEM((E, ROWS, LANES), F32),
            pltpu.VMEM((2, LANES), F32),
            pltpu.VMEM((1, LANES), F32),
            pltpu.VMEM((NR, E, BLOCKS, LANES), F32),
            pltpu.VMEM((E, BLOCKS, LANES), F32),
            pltpu.VMEM((X * Y, NR, 2, LANES), BF16),
            dma((E + 2,)), dma((E, NR - 1)), dma((E, NR)),
            dma((2, STEPS)), dma((STEPS,)), dma((STEPS,)),
            dma((3, STEPS)), dma((2, STEPS)), dma((K,)),
            dma((NR - 1,)), dma((NR,)), dma((X - 1,)), dma((X,)), dma((Y - 1,)), dma((Y,)),
        ],
        compiler_params=pltpu.CompilerParams(
            collective_id=0, has_side_effects=True, vmem_limit_bytes=24 * 1024 * 1024
        ),
    )(*(pltpu.with_memory_space_constraint(a, pltpu.HBM) for a in (w_down, router_weight.T, router_gain[None, :])))
    return out, scale, router.T


def solution(mesh):
    placed = (P("owner", None, "rows"), P("rows", "owner"), P("rows"))
    return jax.shard_map(
        on_device,
        mesh=mesh,
        in_specs=placed,
        out_specs=(P("owner", None, None), P("owner", None), P()),
        check_vma=False,
    )
```

time: 127 us -> 87.9 us (0.69)
  Pallas kernels: 0 us -> 81.3 us
  blocking collectives: 57 us -> 0 us
  waiting for transfers between devices: 41 us -> 0 us
  between operations: 14.1 us -> 0.64 us
  local copies, waits for them, and re-layouts: 11.1 us -> 5.74 us
  other arithmetic: 3.29 us -> 0 us
    pallas_call x0 -> x1, Pallas kernels: none -> 81.3 us  [on_device(): pl.pallas_call(kernel, name='serve', out_shape=(jax.ShapeDtypeStruct((E,...]
    all_to_all x2 -> x0, blocking collectives: 42.3 us -> none  [sent_to_all(): return lax.all_to_all(copies, axis, split_axis=0, concat_axis=0, tiled=True)]
    all_gather x1 -> x0, waiting for transfers between devices: 40.9 us -> none  [on_device(): serve_down = lax.all_gather(narrow_down, 'rows', axis=2, tiled=True)]
    all_gather x1 -> x0, blocking collectives: 14.6 us -> none  [on_device(): row_router = lax.all_gather(part_router, 'rows', axis=0, tiled=True)]
    unnamed x9 -> x3, local copies, waits for them, and re-layouts: 10.1 us -> 5.74 us
    reduce_max x2 -> x0, other arithmetic: 1.98 us -> none  [the longest x1 1.91 us: on_device(): scale_down = of_everyone(jnp.max(jnp.abs(w_down), axis=2), 'rows')]
    convert_element_type x2 -> x0, other arithmetic: 1.31 us -> none  [the longest x1 1.3 us: on_device(): narrow_down = (w_down / jnp.expand_dims(scale_down, 2)).astype(jnp.bfloat16)]
  transfers between devices with their start and end apart: 1 -> 0, of which waited for: 1 -> 0; matrix products, arithmetic and copies ran while one was open for 1% -> 0% of each run, Pallas kernels for 0% -> 0%
where the time goes in v1:
time: 87.9 us; the launch traced here: 87.7 us
  Pallas kernels  81.3 us (92%)
  local copies, waits for them, and re-layouts  5.74 us (7%)
    pallas_call x1, Pallas kernels, on_device(): pl.pallas_call(kernel, name='serve', out_shape=(jax.ShapeDtypeStruct((E,...  81.3 us
    unnamed x3, local copies, waits for them, and re-layouts  5.74 us

profile of v1, /device:TPU:1, one launch (start us, length us, event | category | flops | bytes accessed | tf_op | source)
XLA Modules:
  0.0 87.7 jit_solution(14477810559015170609)
XLA Ops:
  0.6 81.3 %serve.1 = (bf16[2,1408,2048]{2,1,0:T(8,128)(2,1)S(1)}, f32[2,1408]{1,0:T(2,128)S(1)}, bf16[64,2048]{1,0:T(8,128)(2,1)S(1)}) custom-call(f32[2,1408,128]{2,1,0:T(8,128)} %w_hbm.1, f32[2,128]{1,0:T(2,128)} %bitcast.4, f32[1,128]{1,0:T(1,128)} %bitcast.5), custom_call_target="tpu_custom_call" | custom-call | tf_op jit(solution)/shard_map/serve/pallas_call | solution.py:217
  82.0 4.4 %copy.9 = bf16[2,1408,2048]{2,1,0:T(8,128)(2,1)} copy(bf16[2,1408,2048]{2,1,0:T(8,128)(2,1)S(1)} %get-tuple-element.12) | data formatting | bytes 23068672
  86.4 0.6 copy.10
  87.0 0.7 copy.11

commit v2 on v0

v2 whole, which is shorter than its diff:
```python
import jax
import jax.numpy as jnp
from jax import lax
from jax.experimental import pallas as pl
from jax.experimental.pallas import tpu as pltpu
from jax.sharding import PartitionSpec as P

MESH = pl.DeviceIdType.MESH
BF16 = jnp.bfloat16
F32 = jnp.float32

E = 2
ROWS = 1408
LANES = 128
Z = 8
NR = 16
X, Y = 4, 8
PIECES = ((0, 0, 3), (0, 3, 8), (1, 0, 11))
CHUNKS = ((0, 0, 3, 0), (0, 3, 8, 1), (1, 0, 8, 2), (1, 8, 3, 2))
K = len(CHUNKS)
ARRIVALS = tuple(
    tuple((d, k) for d in range(3) for k in range(K)) + tuple((3, k) for k in far)
    for far in ((1, 0), (2, 3))
)
STEPS = len(ARRIVALS[0])


def kernel(w_hbm, rw_hbm, gain_hbm, out, scale_out, router_out,
           w, rw, gain, mx0, mx1, mx2, mine, rb,
           in_sem, go, mx_send, mx_recv, ring_send, right_recv, left_recv,
           die_send, die_recv, own_send, own_recv,
           r1_send, r1_recv, rx_send, rx_recv, ry_send, ry_recv, rd_send, rd_recv):
    owner = lax.axis_index("owner")
    rows = lax.axis_index("rows")
    z, core = rows // 2, rows % 2
    x, y = owner % X, owner // X
    barrier = pltpu.get_barrier_semaphore()
    first_core, second_core = core == 0, core == 1
    mx = (mx0, mx1, mx2)

    column = [(rows + d) % NR for d in range(1, NR)]
    chips = [(z + d) % Z for d in range(1, Z)]
    across_x = [y * X + (x + d) % X for d in range(1, X)]
    across_y = [((y + d) % Y) * X + x for d in range(1, Y)]
    right = ((z + 1) % Z) * 2 + core
    left = ((z + Z - 1) % Z) * 2 + core
    partner = z * 2 + 1 - core

    def remote(src, dst, send, recv, **where):
        return pltpu.make_async_remote_copy(
            src_ref=src, dst_ref=dst, send_sem=send, recv_sem=recv,
            device_id=where, device_id_type=MESH)

    def signal(sem, **where):
        pl.semaphore_signal(sem, inc=1, device_id=where, device_id_type=MESH)

    for c in chips:
        signal(barrier, rows=c * 2)

    @pl.when(second_core)
    def _():
        signal(barrier, rows=partner)
        for o in across_x + across_y:
            signal(barrier, owner=o)

    spans = [(e, b * LANES, n * LANES) for e, b, n in PIECES]
    loads = [
        pltpu.make_async_copy(w_hbm.at[e, pl.ds(a, n)], w.at[e, pl.ds(a, n)], in_sem.at[i])
        for i, (e, a, n) in enumerate(spans)
    ]
    loads.append(pltpu.make_async_copy(rw_hbm, rw, in_sem.at[3]))
    loads.append(pltpu.make_async_copy(gain_hbm, gain, in_sem.at[4]))
    for load in loads:
        load.start()

    def maxima(i):
        loads[i].wait()
        e, first, n = PIECES[i]
        for b in range(n):
            block = jnp.abs(w[e, (first + b) * LANES:(first + b + 1) * LANES, :])
            mx[i][rows, b:b + 1, :] = jnp.max(block.T, axis=0, keepdims=True)

    def mx_copies(i):
        return [
            remote(mx[i].at[rows], mx[i].at[rows], mx_send.at[i, s], mx_recv.at[i, rows], rows=r)
            for s, r in enumerate(column)
        ]

    sent = [mx_copies(i) for i in range(3)]
    maxima(0)

    @pl.when(first_core)
    def _():
        pl.semaphore_wait(barrier, NR - 1)
        signal(go, rows=partner)

    @pl.when(second_core)
    def _():
        pl.semaphore_wait(go, 1)

    for copy in sent[0]:
        copy.start()
    for i in (1, 2):
        maxima(i)
        for copy in sent[i]:
            copy.start()

    loads[3].wait()
    loads[4].wait()
    piece = (rw[...] * gain[...]).astype(BF16)
    mine[...] = piece
    r1 = [remote(mine, rb.at[owner, rows], r1_send.at[s], r1_recv.at[rows], rows=c * 2 + 1) for s, c in enumerate(chips)]
    r1_die = remote(mine, rb.at[owner, rows], r1_send.at[Z - 1], r1_recv.at[rows], rows=partner)
    for copy in r1:
        copy.start()

    @pl.when(first_core)
    def _():
        r1_die.start()

    @pl.when(second_core)
    def _():
        rb[owner, rows] = piece

    def cells(origin, k):
        e, first, n, _ = CHUNKS[k]
        lanes = pl.multiple_of(origin * LANES, LANES)
        return out.at[e, pl.ds(first * LANES, n * LANES), pl.ds(lanes, LANES)]

    def ring(side, origin, k, sent_at, recv_at):
        part = cells(origin, k)
        recv = (right_recv, left_recv)[side]
        return remote(part, part, ring_send.at[side, sent_at], recv.at[recv_at], rows=(right, left)[side])

    def die(side, origin, k, j):
        part = cells(origin, k)
        return remote(part, part, die_send.at[side, j], die_recv.at[side, j], rows=partner)

    def die_own(origin, k):
        part = cells(origin, k)
        return remote(part, part, own_send.at[k], own_recv.at[k], rows=partner)

    def scaled(i):
        for s, r in enumerate(column):
            remote(mx[i].at[r], mx[i].at[r], mx_send.at[i, s], mx_recv.at[i, r], rows=r).wait_recv()
        scale = jnp.max(mx[i][...], axis=0)
        e, first, n = PIECES[i]
        for b in range(n):
            scale_out[e:e + 1, (first + b) * LANES:(first + b + 1) * LANES] = scale[b:b + 1]
        return 1.0 / scale

    inv = None
    held = -1
    for k, (e, first, n, i) in enumerate(CHUNKS):
        if i != held:
            inv, held = scaled(i), i
        skip = first - PIECES[i][1]
        lanes = pl.ds(pl.multiple_of(rows * LANES, LANES), LANES)
        for b in range(n):
            factor = jnp.broadcast_to(inv[skip + b:skip + b + 1], (LANES, LANES)).T
            span = slice((first + b) * LANES, (first + b + 1) * LANES)
            out[e, span, lanes] = (w[e, span, :] * factor).astype(BF16)
        for side in range(2):
            ring(side, rows, k, k, k).start()
        die_own(rows, k).start()

    def origin_of(side, d, c):
        step = (Z - 1 - d) if side == 0 else (d + 1)
        return ((z + step) % Z) * 2 + c

    def arrive(j):
        for side in range(2):
            d, k = ARRIVALS[side][j]
            origin = origin_of(side, d, core)
            ring(side, origin, k, j, j).wait_recv()
            onward = [(d + 1, k)] if d < 2 else []
            if d == 2:
                onward = {(0, 1): [(3, 1), (3, 0)], (1, 2): [(3, 2)], (1, 3): [(3, 3)]}.get((side, k), [])
            for to in onward:
                at = ARRIVALS[side].index(to)
                ring(side, origin, to[1], at, at).start()
            die(side, origin, k, j).start()

    rx = [remote(rb.at[owner], rb.at[owner], rx_send.at[s], rx_recv.at[x], owner=o) for s, o in enumerate(across_x)]
    band = rb.at[pl.ds(y * X, X)]
    ry = [remote(band, band, ry_send.at[s], ry_recv.at[y], owner=o) for s, o in enumerate(across_y)]
    rd = remote(rb, rb, rd_send, rd_recv, rows=partner)

    def router_x():
        @pl.when(second_core)
        def _():
            for s, r in enumerate(column):
                remote(mine, rb.at[owner, r], r1_send.at[0], r1_recv.at[r], rows=r).wait_recv()
            pl.semaphore_wait(barrier, len(across_x) + len(across_y))
            for copy in rx:
                copy.start()

    def router_y():
        @pl.when(second_core)
        def _():
            for o in across_x:
                remote(rb.at[o], rb.at[o], rx_send.at[0], rx_recv.at[o % X], owner=o).wait_recv()
            for copy in ry:
                copy.start()

    def router_die():
        @pl.when(second_core)
        def _():
            for o in across_y:
                theirs = rb.at[pl.ds((o // X) * X, X)]
                remote(theirs, theirs, ry_send.at[0], ry_recv.at[o // X], owner=o).wait_recv()
            rd.start()

    def router_end():
        @pl.when(first_core)
        def _():
            rd.wait_recv()

        for o in range(X * Y):
            for r in range(NR):
                router_out[2 * o:2 * o + 2, r * LANES:(r + 1) * LANES] = rb[o, r]

    between = {4: router_x, 6: router_y, 8: router_die, 10: router_end}
    for j in range(STEPS):
        if j in between:
            between[j]()
        arrive(j)

    for k in range(K):
        die_own(partner, k).wait_recv()
        die_own(rows, k).wait_send()
    for j in range(STEPS):
        for side in range(2):
            d, k = ARRIVALS[side][j]
            die(side, origin_of(side, d, 1 - core), k, j).wait_recv()
    for j in range(STEPS):
        for side in range(2):
            d, k = ARRIVALS[side][j]
            die(side, origin_of(side, d, core), k, j).wait_send()
    for side in range(2):
        for k in range(K):
            ring(side, rows, k, k, k).wait_send()
        for at in range(K, STEPS):
            d, k = ARRIVALS[side][at]
            ring(side, origin_of(side, d - 1, core), k, at, at).wait_send()
    for copies in sent:
        for copy in copies:
            copy.wait_send()
    for copy in r1:
        copy.wait_send()

    @pl.when(first_core)
    def _():
        r1_die.wait_send()

    @pl.when(second_core)
    def _():
        for copy in rx + ry + [rd]:
            copy.wait_send()


PARTS = 11


def write(a, b, c, a_out, b_out, c_out, sems):
    tall = ROWS // PARTS
    copies = [
        pltpu.make_async_copy(a.at[e, pl.ds(i * tall, tall)], a_out.at[e, pl.ds(i * tall, tall)], sems.at[e * PARTS + i])
        for e in range(E) for i in range(PARTS)
    ]
    copies.append(pltpu.make_async_copy(b, b_out, sems.at[E * PARTS]))
    copies.append(pltpu.make_async_copy(c, c_out, sems.at[E * PARTS + 1]))
    for copy in copies:
        copy.start()
    for copy in copies:
        copy.wait()


def on_device(w_down, router_weight, router_gain):
    dma = pltpu.SemaphoreType.DMA
    shapes = (
        jax.ShapeDtypeStruct((E, ROWS, NR * LANES), BF16),
        jax.ShapeDtypeStruct((E, ROWS), F32),
        jax.ShapeDtypeStruct((E * X * Y, NR * LANES), BF16),
    )
    args = (w_down, router_weight.T, router_gain[None, :])
    held = pl.pallas_call(
        kernel,
        name="serve",
        out_shape=shapes,
        in_specs=[pl.BlockSpec(memory_space=pltpu.HBM)] * 3,
        out_specs=(pl.BlockSpec(memory_space=pltpu.VMEM),) * 3,
        scratch_shapes=[
            pltpu.VMEM((E, ROWS, LANES), F32),
            pltpu.VMEM((2, LANES), F32),
            pltpu.VMEM((1, LANES), F32),
            *[pltpu.VMEM((NR, n, LANES), F32) for _, _, n in PIECES],
            pltpu.VMEM((2, LANES), BF16),
            pltpu.VMEM((X * Y, NR, 2, LANES), BF16),
            dma((5,)), pltpu.SemaphoreType.REGULAR, dma((3, NR - 1)), dma((3, NR)),
            dma((2, STEPS)), dma((STEPS,)), dma((STEPS,)),
            dma((2, STEPS)), dma((2, STEPS)), dma((K,)), dma((K,)),
            dma((Z,)), dma((NR,)), dma((X - 1,)), dma((X,)), dma((Y - 1,)), dma((Y,)), dma(()), dma(()),
        ],
        compiler_params=pltpu.CompilerParams(
            collective_id=0, has_side_effects=True, vmem_limit_bytes=24 * 1024 * 1024
        ),
    )(*(pltpu.with_memory_space_constraint(a, pltpu.HBM) for a in args))
    out, scale, router = pl.pallas_call(
        write,
        name="write",
        out_shape=shapes,
        in_specs=[pl.BlockSpec(memory_space=pltpu.VMEM)] * 3,
        out_specs=(pl.BlockSpec(memory_space=pltpu.HBM),) * 3,
        scratch_shapes=[dma((E * PARTS + 2,))],
        compiler_params=pltpu.CompilerParams(vmem_limit_bytes=24 * 1024 * 1024),
    )(*held)
    return out, scale, router.T


def solution(mesh):
    placed = (P("owner", None, "rows"), P("rows", "owner"), P("rows"))
    return jax.shard_map(
        on_device,
        mesh=mesh,
        in_specs=placed,
        out_specs=(P("owner", None, None), P("owner", None), P()),
        check_vma=False,
    )
```

time: 127 us -> 83 us (0.65)
  Pallas kernels: 0 us -> 82.2 us
  blocking collectives: 57 us -> 0 us
  waiting for transfers between devices: 41 us -> 0 us
  between operations: 14.1 us -> 0.64 us
  local copies, waits for them, and re-layouts: 11.1 us -> 0 us
  other arithmetic: 3.29 us -> 0 us
    pallas_call x0 -> x2, Pallas kernels: none -> 82.2 us  [the longest x1 77.7 us: on_device(): pl.pallas_call(kernel, name='serve', out_shape=shapes, in_specs=[pl.Block...]
    all_to_all x2 -> x0, blocking collectives: 42.3 us -> none  [sent_to_all(): return lax.all_to_all(copies, axis, split_axis=0, concat_axis=0, tiled=True)]
    all_gather x1 -> x0, waiting for transfers between devices: 40.9 us -> none  [on_device(): serve_down = lax.all_gather(narrow_down, 'rows', axis=2, tiled=True)]
    all_gather x1 -> x0, blocking collectives: 14.6 us -> none  [on_device(): row_router = lax.all_gather(part_router, 'rows', axis=0, tiled=True)]
    unnamed x9 -> x0, local copies, waits for them, and re-layouts: 10.1 us -> none
    reduce_max x2 -> x0, other arithmetic: 1.98 us -> none  [the longest x1 1.91 us: on_device(): scale_down = of_everyone(jnp.max(jnp.abs(w_down), axis=2), 'rows')]
    convert_element_type x2 -> x0, other arithmetic: 1.31 us -> none  [the longest x1 1.3 us: on_device(): narrow_down = (w_down / jnp.expand_dims(scale_down, 2)).astype(jnp.bfloat16)]
  transfers between devices with their start and end apart: 1 -> 0, of which waited for: 1 -> 0; matrix products, arithmetic and copies ran while one was open for 1% -> 0% of each run, Pallas kernels for 0% -> 0%
where the time goes in v2:
time: 83 us; the launch traced here: 82.8 us
  Pallas kernels  82.2 us (99%)
    pallas_call x1, Pallas kernels, on_device(): pl.pallas_call(kernel, name='serve', out_shape=shapes, in_specs=[pl.Block...  77.7 us
    pallas_call x1, Pallas kernels, on_device(): pl.pallas_call(write, name='write', out_shape=shapes, in_specs=[pl.BlockS...  4.5 us

profile of v2, /device:TPU:1, one launch (start us, length us, event | category | flops | bytes accessed | tf_op | source)
XLA Modules:
  0.0 82.8 jit_solution(18241954555974672769)
XLA Ops:
  0.6 77.7 %serve.1 = (bf16[2,1408,2048]{2,1,0:T(8,128)(2,1)S(1)}, f32[2,1408]{1,0:T(2,128)S(1)}, bf16[64,2048]{1,0:T(8,128)(2,1)S(1)}) custom-call(f32[2,1408,128]{2,1,0:T(8,128)} %w_hbm.1, f32[2,128]{1,0:T(2,128)} %bitcast.3, f32[1,128]{1,0:T(1,128)} %bitcast.4), custom_call_target="tpu_custom_call" | custom-call | tf_op jit(solution)/shard_map/serve/pallas_call | solution.py:287
  78.3 4.5 %write.1 = (bf16[2,1408,2048]{2,1,0:T(8,128)(2,1)}, f32[2,1408]{1,0:T(2,128)}, bf16[64,2048]{1,0:T(8,128)(2,1)}) custom-call(bf16[2,1408,2048]{2,1,0:T(8,128)(2,1)S(1)} %get-tuple-element.9.a, f32[2,1408]{1,0:T(2,128)S(1)} %get-tuple-element.10.b, bf16[64,2048]{1,0:T(8,128)(2,1)S(1)} %get-tuple-element.11.c), custom_call_target="tpu_custom_call" | custom-call | tf_op jit(solution)/shard_map/write/pallas_call | solution.py:309

commit v3 on v2

v3 whole, which is shorter than its diff:
```python
import jax
import jax.numpy as jnp
from jax import lax
from jax.experimental import pallas as pl
from jax.experimental.pallas import tpu as pltpu
from jax.sharding import PartitionSpec as P

MESH = pl.DeviceIdType.MESH
BF16 = jnp.bfloat16
F32 = jnp.float32

E = 2
ROWS = 1408
LANES = 128
Z = 8
NR = 16
X, Y = 4, 8
BLOCKS = ROWS // LANES
HALF = 6
CHUNKS = ((0, 0, 3), (0, 3, 8), (1, 0, 8), (1, 8, 3))
K = len(CHUNKS)
RAW = CHUNKS[0][2] * LANES
NEAR = ((0, 1), (1, 0), (0, 2), (0, 3), (1, 1), (2, 0), (1, 2), (1, 3), (2, 1), (2, 2), (2, 3))
ARRIVALS = (NEAR + ((3, 1), (3, 0)), NEAR + ((3, 2), (3, 3)))
FAR = ({1: ((3, 1), (3, 0))}, {2: ((3, 2),), 3: ((3, 3),)})


def kernel(w_hbm, rw_hbm, gain_hbm, out, scale_out, router_out,
           w, rw, gain, mx, half, swapped, reduced, final, raw, mine, rb,
           in_sem, go, mx_send, mx_recv, sw_send, sw_recv, red_send, red_recv, fin_send, fin_recv,
           raw_send, raw_recv, ring_send, right_recv, left_recv,
           die_send, die_recv, own_send, own_recv,
           r1_send, r1_recv, rx_send, rx_recv, ry_send, ry_recv, rd_send, rd_recv):
    owner = lax.axis_index("owner")
    rows = lax.axis_index("rows")
    z, core = rows // 2, rows % 2
    x, y = owner % X, owner // X
    barrier = pltpu.get_barrier_semaphore()
    first_core, second_core = core == 0, core == 1

    column = [(rows + d) % NR for d in range(1, NR)]
    chips = [(z + d) % Z for d in range(1, Z)]
    across_x = [y * X + (x + d) % X for d in range(1, X)]
    across_y = [((y + d) % Y) * X + x for d in range(1, Y)]
    sides = (((z + 1) % Z) * 2 + core, ((z + Z - 1) % Z) * 2 + core)
    partner = z * 2 + 1 - core

    def remote(src, dst, send, recv, **where):
        return pltpu.make_async_remote_copy(
            src_ref=src, dst_ref=dst, send_sem=send, recv_sem=recv,
            device_id=where, device_id_type=MESH)

    def signal(sem, **where):
        pl.semaphore_signal(sem, inc=1, device_id=where, device_id_type=MESH)

    for c in chips:
        signal(barrier, rows=c * 2)

    @pl.when(second_core)
    def _():
        signal(barrier, rows=partner)
        for o in across_x + across_y:
            signal(barrier, owner=o)

    loads = [pltpu.make_async_copy(w_hbm.at[e], w.at[e], in_sem.at[e]) for e in range(E)]
    loads.append(pltpu.make_async_copy(rw_hbm, rw, in_sem.at[2]))
    loads.append(pltpu.make_async_copy(gain_hbm, gain, in_sem.at[3]))
    for load in loads:
        load.start()

    def span(b):
        return slice(b * LANES, (b + 1) * LANES)

    def maximum(e, b):
        return jnp.max(jnp.abs(w[e, span(b), :]).T, axis=0, keepdims=True)

    loads[0].wait()
    for b in range(BLOCKS):
        mx[rows, b:b + 1, :] = maximum(0, b)

    @pl.when(first_core)
    def _():
        pl.semaphore_wait(barrier, NR - 1)
        signal(go, rows=partner)

    @pl.when(second_core)
    def _():
        pl.semaphore_wait(go, 1)

    mx_sent = [remote(mx.at[rows], mx.at[rows], mx_send.at[s], mx_recv.at[rows], rows=r) for s, r in enumerate(column)]
    for copy in mx_sent:
        copy.start()
    raw_sent = [
        remote(w.at[0, pl.ds(0, RAW)], raw.at[side], raw_send.at[side], raw_recv.at[side], rows=sides[side])
        for side in range(2)
    ]
    for copy in raw_sent:
        copy.start()

    loads[1].wait()
    for b in range(BLOCKS):
        top = maximum(1, b)
        for h, first in enumerate((0, BLOCKS - HALF)):
            if first <= b < first + HALF:
                half[h, b - first:b - first + 1, :] = top
    swap = remote(half.at[1 - core], swapped, sw_send, sw_recv, rows=partner)
    swap.start()

    loads[2].wait()
    loads[3].wait()
    piece = (rw[...] * gain[...]).astype(BF16)
    mine[...] = piece
    r1 = [remote(mine, rb.at[owner, rows], r1_send.at[s], r1_recv.at[rows], rows=c * 2 + 1) for s, c in enumerate(chips)]
    r1_die = remote(mine, rb.at[owner, rows], r1_send.at[Z - 1], r1_recv.at[rows], rows=partner)
    for copy in r1:
        copy.start()

    @pl.when(first_core)
    def _():
        r1_die.start()

    @pl.when(second_core)
    def _():
        rb[owner, rows] = piece

    swap.wait_recv()
    reduced[z] = jnp.maximum(half[core], swapped[...])
    red_sent = [remote(reduced.at[z], reduced.at[z], red_send.at[s], red_recv.at[z], rows=c * 2 + core) for s, c in enumerate(chips)]
    for copy in red_sent:
        copy.start()

    def cells(origin, k):
        e, first, n = CHUNKS[k]
        lanes = pl.multiple_of(origin * LANES, LANES)
        return out.at[e, pl.ds(first * LANES, n * LANES), pl.ds(lanes, LANES)]

    def ring(side, origin, to):
        d, k = to
        part = cells(origin, k)
        recv = (right_recv, left_recv)[side]
        return remote(part, part, ring_send.at[side, d * K + k], recv.at[d * K + k], rows=sides[side])

    def die(side, origin, at):
        d, k = at
        part = cells(origin, k)
        return remote(part, part, die_send.at[side, d * K + k], die_recv.at[side, d * K + k], rows=partner)

    def die_own(origin, k):
        part = cells(origin, k)
        return remote(part, part, own_send.at[k], own_recv.at[k], rows=partner)

    def origin_of(side, d, c):
        step = (Z - 1 - d) if side == 0 else (d + 1)
        return ((z + step) % Z) * 2 + c

    def narrow(values, origin, k, factors):
        e, first, n = CHUNKS[k]
        lanes = pl.ds(pl.multiple_of(origin * LANES, LANES), LANES)
        for b in range(n):
            factor = jnp.broadcast_to(factors[first + b], (LANES, LANES)).T
            out[e, span(first + b), lanes] = (values(e, first + b) * factor).astype(BF16)

    def own(k, factors):
        narrow(lambda e, b: w[e, span(b), :], rows, k, factors)
        if k > 0:
            for side in range(2):
                ring(side, rows, (0, k)).start()
        die_own(rows, k).start()

    def scaled(e, tops):
        for b in range(BLOCKS):
            scale_out[e:e + 1, span(b)] = tops[b]
        return [1.0 / top for top in tops]

    for s, r in enumerate(column):
        remote(mx.at[r], mx.at[r], mx_send.at[s], mx_recv.at[r], rows=r).wait_recv()
    top = jnp.max(mx[...], axis=0)
    factors = scaled(0, [top[b:b + 1] for b in range(BLOCKS)])
    own(1, factors)
    own(0, factors)
    for side in range(2):
        origin = origin_of(side, 0, core)
        raw_sent[side].wait_recv()
        narrow(lambda e, b: raw[side, span(b), :], origin, 0, factors)
        ring(side, origin, (1, 0)).start()
        die(side, origin, (0, 0)).start()

    for s, c in enumerate(chips):
        remote(reduced.at[c], reduced.at[c], red_send.at[s], red_recv.at[c], rows=c * 2 + core).wait_recv()
    final[core] = jnp.max(reduced[...], axis=0)
    share = remote(final.at[core], final.at[core], fin_send, fin_recv, rows=partner)
    share.start()
    remote(final.at[1 - core], final.at[1 - core], fin_send, fin_recv, rows=partner).wait_recv()
    low, high = final[0], final[1]
    tops = [low[b:b + 1] for b in range(HALF)]
    tops += [high[b - BLOCKS + HALF:b - BLOCKS + HALF + 1] for b in range(HALF, BLOCKS)]
    factors = scaled(1, tops)
    own(2, factors)
    own(3, factors)

    def arrive(j):
        for side in range(2):
            d, k = ARRIVALS[side][j]
            origin = origin_of(side, d, core)
            ring(side, origin, (d, k)).wait_recv()
            onward = ((d + 1, k),) if d < 2 else FAR[side].get(k, ()) if d == 2 else ()
            for to in onward:
                ring(side, origin, to).start()
            die(side, origin, (d, k)).start()

    rx = [remote(rb.at[owner], rb.at[owner], rx_send.at[s], rx_recv.at[x], owner=o) for s, o in enumerate(across_x)]
    band = rb.at[pl.ds(y * X, X)]
    ry = [remote(band, band, ry_send.at[s], ry_recv.at[y], owner=o) for s, o in enumerate(across_y)]
    rd = remote(rb, rb, rd_send, rd_recv, rows=partner)

    def router_x():
        @pl.when(second_core)
        def _():
            for s, r in enumerate(column):
                remote(mine, rb.at[owner, r], r1_send.at[0], r1_recv.at[r], rows=r).wait_recv()
            pl.semaphore_wait(barrier, len(across_x) + len(across_y))
            for copy in rx:
                copy.start()

    def router_y():
        @pl.when(second_core)
        def _():
            for o in across_x:
                remote(rb.at[o], rb.at[o], rx_send.at[0], rx_recv.at[o % X], owner=o).wait_recv()
            for copy in ry:
                copy.start()

    def router_die():
        @pl.when(second_core)
        def _():
            for o in across_y:
                theirs = rb.at[pl.ds((o // X) * X, X)]
                remote(theirs, theirs, ry_send.at[0], ry_recv.at[o // X], owner=o).wait_recv()
            rd.start()

    def router_end():
        @pl.when(first_core)
        def _():
            rd.wait_recv()

        for o in range(X * Y):
            for r in range(NR):
                router_out[2 * o:2 * o + 2, r * LANES:(r + 1) * LANES] = rb[o, r]

    between = {3: router_x, 5: router_y, 7: router_die, 9: router_end}
    for j in range(len(NEAR) + 2):
        if j in between:
            between[j]()
        arrive(j)

    for k in range(K):
        die_own(partner, k).wait_recv()
    for side in range(2):
        for d, k in ((0, 0),) + ARRIVALS[side]:
            die(side, origin_of(side, d, 1 - core), (d, k)).wait_recv()
    for k in range(K):
        die_own(rows, k).wait_send()
    for side in range(2):
        raw_sent[side].wait_send()
        die(side, origin_of(side, 0, core), (0, 0)).wait_send()
        for d, k in ARRIVALS[side]:
            die(side, origin_of(side, d, core), (d, k)).wait_send()
            ring(side, origin_of(side, d - 1, core), (d, k)).wait_send()
    for copy in mx_sent + red_sent + r1 + [swap, share]:
        copy.wait_send()

    @pl.when(first_core)
    def _():
        r1_die.wait_send()

    @pl.when(second_core)
    def _():
        for copy in rx + ry + [rd]:
            copy.wait_send()


PARTS = 11


def write(a, b, c, a_out, b_out, c_out, sems):
    tall = ROWS // PARTS
    copies = [
        pltpu.make_async_copy(a.at[e, pl.ds(i * tall, tall)], a_out.at[e, pl.ds(i * tall, tall)], sems.at[e * PARTS + i])
        for e in range(E) for i in range(PARTS)
    ]
    copies.append(pltpu.make_async_copy(b, b_out, sems.at[E * PARTS]))
    copies.append(pltpu.make_async_copy(c, c_out, sems.at[E * PARTS + 1]))
    for copy in copies:
        copy.start()
    for copy in copies:
        copy.wait()


def on_device(w_down, router_weight, router_gain):
    dma = pltpu.SemaphoreType.DMA
    shapes = (
        jax.ShapeDtypeStruct((E, ROWS, NR * LANES), BF16),
        jax.ShapeDtypeStruct((E, ROWS), F32),
        jax.ShapeDtypeStruct((E * X * Y, NR * LANES), BF16),
    )
    args = (w_down, router_weight.T, router_gain[None, :])
    held = pl.pallas_call(
        kernel,
        name="serve",
        out_shape=shapes,
        in_specs=[pl.BlockSpec(memory_space=pltpu.HBM)] * 3,
        out_specs=(pl.BlockSpec(memory_space=pltpu.VMEM),) * 3,
        scratch_shapes=[
            pltpu.VMEM((E, ROWS, LANES), F32),
            pltpu.VMEM((2, LANES), F32),
            pltpu.VMEM((1, LANES), F32),
            pltpu.VMEM((NR, BLOCKS, LANES), F32),
            pltpu.VMEM((2, HALF, LANES), F32),
            pltpu.VMEM((HALF, LANES), F32),
            pltpu.VMEM((Z, HALF, LANES), F32),
            pltpu.VMEM((2, HALF, LANES), F32),
            pltpu.VMEM((2, RAW, LANES), F32),
            pltpu.VMEM((2, LANES), BF16),
            pltpu.VMEM((X * Y, NR, 2, LANES), BF16),
            dma((4,)), pltpu.SemaphoreType.REGULAR, dma((NR - 1,)), dma((NR,)),
            dma(()), dma(()), dma((Z - 1,)), dma((Z,)), dma(()), dma(()),
            dma((2,)), dma((2,)), dma((2, 4 * K)), dma((4 * K,)), dma((4 * K,)),
            dma((2, 4 * K)), dma((2, 4 * K)), dma((K,)), dma((K,)),
            dma((Z,)), dma((NR,)), dma((X - 1,)), dma((X,)), dma((Y - 1,)), dma((Y,)), dma(()), dma(()),
        ],
        compiler_params=pltpu.CompilerParams(
            collective_id=0, has_side_effects=True, vmem_limit_bytes=24 * 1024 * 1024
        ),
    )(*(pltpu.with_memory_space_constraint(a, pltpu.HBM) for a in args))
    out, scale, router = pl.pallas_call(
        write,
        name="write",
        out_shape=shapes,
        in_specs=[pl.BlockSpec(memory_space=pltpu.VMEM)] * 3,
        out_specs=(pl.BlockSpec(memory_space=pltpu.HBM),) * 3,
        scratch_shapes=[dma((E * PARTS + 2,))],
        compiler_params=pltpu.CompilerParams(vmem_limit_bytes=24 * 1024 * 1024),
    )(*held)
    return out, scale, router.T


def solution(mesh):
    placed = (P("owner", None, "rows"), P("rows", "owner"), P("rows"))
    return jax.shard_map(
        on_device,
        mesh=mesh,
        in_specs=placed,
        out_specs=(P("owner", None, None), P("owner", None), P()),
        check_vma=False,
    )
```

time: 83 us -> 81.4 us (0.981)
  Pallas kernels: 82.2 us -> 80.7 us
    pallas_call x1, Pallas kernels: 77.7 us -> 76.2 us  [on_device(): pl.pallas_call(kernel, name='serve', out_shape=shapes, in_specs=[pl.Block...]
where the time goes in v3:
time: 81.4 us; the launch traced here: 81.3 us
  Pallas kernels  80.7 us (99%)
    pallas_call x1, Pallas kernels, on_device(): pl.pallas_call(kernel, name='serve', out_shape=shapes, in_specs=[pl.Block...  76.2 us
    pallas_call x1, Pallas kernels, on_device(): pl.pallas_call(write, name='write', out_shape=shapes, in_specs=[pl.BlockS...  4.5 us

profile of v3, /device:TPU:1, one launch (start us, length us, event | category | flops | bytes accessed | tf_op | source)
XLA Modules:
  0.0 81.3 jit_solution(1653844195488510704)
XLA Ops:
  0.6 76.2 %serve.1 = (bf16[2,1408,2048]{2,1,0:T(8,128)(2,1)S(1)}, f32[2,1408]{1,0:T(2,128)S(1)}, bf16[64,2048]{1,0:T(8,128)(2,1)S(1)}) custom-call(f32[2,1408,128]{2,1,0:T(8,128)} %w_hbm.1, f32[2,128]{1,0:T(2,128)} %bitcast.3, f32[1,128]{1,0:T(1,128)} %bitcast.4), custom_call_target="tpu_custom_call" | custom-call | tf_op jit(solution)/shard_map/serve/pallas_call | solution.py:307
  76.8 4.5 %write.1 = (bf16[2,1408,2048]{2,1,0:T(8,128)(2,1)}, f32[2,1408]{1,0:T(2,128)}, bf16[64,2048]{1,0:T(8,128)(2,1)}) custom-call(bf16[2,1408,2048]{2,1,0:T(8,128)(2,1)S(1)} %get-tuple-element.9.a, f32[2,1408]{1,0:T(2,128)S(1)} %get-tuple-element.10.b, bf16[64,2048]{1,0:T(8,128)(2,1)S(1)} %get-tuple-element.11.c), custom_call_target="tpu_custom_call" | custom-call | tf_op jit(solution)/shard_map/write/pallas_call | solution.py:335

commit v4 on v3

--- a/solution.py
+++ b/solution.py
@@ -22,12 +22,14 @@
 RAW = CHUNKS[0][2] * LANES
 NEAR = ((0, 1), (1, 0), (0, 2), (0, 3), (1, 1), (2, 0), (1, 2), (1, 3), (2, 1), (2, 2), (2, 3))
 ARRIVALS = (NEAR + ((3, 1), (3, 0)), NEAR + ((3, 2), (3, 3)))
+STEPS = len(NEAR) + 2
+SETTLED = STEPS - 5
 FAR = ({1: ((3, 1), (3, 0))}, {2: ((3, 2),), 3: ((3, 3),)})
 
 
 def kernel(w_hbm, rw_hbm, gain_hbm, out, scale_out, router_out,
-           w, rw, gain, mx, half, swapped, reduced, final, raw, mine, rb,
-           in_sem, go, mx_send, mx_recv, sw_send, sw_recv, red_send, red_recv, fin_send, fin_recv,
+           w, rw, gain, mx, cross, both, half, swapped, reduced, final, raw, mine, rb,
+           in_sem, go, mx_send, mx_recv, both_send, both_recv, sw_send, sw_recv, red_send, red_recv, fin_send, fin_recv,
            raw_send, raw_recv, ring_send, right_recv, left_recv,
            die_send, die_recv, own_send, own_recv,
            r1_send, r1_recv, rx_send, rx_recv, ry_send, ry_recv, rd_send, rd_recv):
@@ -38,8 +40,8 @@
     barrier = pltpu.get_barrier_semaphore()
     first_core, second_core = core == 0, core == 1
 
+    chips = [(z + d) % Z for d in (4, 3, 5, 2, 6, 1, 7)]
     column = [(rows + d) % NR for d in range(1, NR)]
-    chips = [(z + d) % Z for d in range(1, Z)]
     across_x = [y * X + (x + d) % X for d in range(1, X)]
     across_y = [((y + d) % Y) * X + x for d in range(1, Y)]
     sides = (((z + 1) % Z) * 2 + core, ((z + Z - 1) % Z) * 2 + core)
@@ -76,7 +78,7 @@
 
     loads[0].wait()
     for b in range(BLOCKS):
-        mx[rows, b:b + 1, :] = maximum(0, b)
+        mx[z, b:b + 1, :] = maximum(0, b)
 
     @pl.when(first_core)
     def _():
@@ -87,7 +89,8 @@
     def _():
         pl.semaphore_wait(go, 1)
 
-    mx_sent = [remote(mx.at[rows], mx.at[rows], mx_send.at[s], mx_recv.at[rows], rows=r) for s, r in enumerate(column)]
+    mx_sent = [remote(mx.at[z], mx.at[z], mx_send.at[s], mx_recv.at[z], rows=c * 2 + core) for s, c in enumerate(chips)]
+    mx_sent.insert(1, remote(mx.at[z], cross, mx_send.at[Z - 1], mx_recv.at[Z], rows=chips[0] * 2 + 1 - core))
     for copy in mx_sent:
         copy.start()
     raw_sent = [
@@ -172,9 +175,20 @@
             scale_out[e:e + 1, span(b)] = tops[b]
         return [1.0 / top for top in tops]
 
-    for s, r in enumerate(column):
-        remote(mx.at[r], mx.at[r], mx_send.at[s], mx_recv.at[r], rows=r).wait_recv()
-    top = jnp.max(mx[...], axis=0)
+    def mx_wait(s, c):
+        remote(mx.at[c], mx.at[c], mx_send.at[s], mx_recv.at[c], rows=c * 2 + core).wait_recv()
+
+    near = mx[z]
+    for s, c in list(enumerate(chips))[:0:-1]:
+        mx_wait(s, c)
+        near = jnp.maximum(near, mx[c])
+    both[core] = near
+    meet = remote(both.at[core], both.at[core], both_send, both_recv, rows=partner)
+    meet.start()
+    mx_wait(0, chips[0])
+    remote(cross, cross, mx_send.at[Z - 1], mx_recv.at[Z], rows=partner).wait_recv()
+    remote(both.at[1 - core], both.at[1 - core], both_send, both_recv, rows=partner).wait_recv()
+    top = jnp.maximum(jnp.maximum(both[0], both[1]), jnp.maximum(mx[chips[0]], cross[...]))
     factors = scaled(0, [top[b:b + 1] for b in range(BLOCKS)])
     own(1, factors)
     own(0, factors)
@@ -248,38 +262,54 @@
                 router_out[2 * o:2 * o + 2, r * LANES:(r + 1) * LANES] = rb[o, r]
 
     between = {3: router_x, 5: router_y, 7: router_die, 9: router_end}
-    for j in range(len(NEAR) + 2):
+    def settle(side, at):
+        d, k = at
+        die(side, origin_of(side, d, 1 - core), at).wait_recv()
+        die(side, origin_of(side, d, core), at).wait_send()
+
+    def sent(side, at):
+        d, k = at
+        ring(side, origin_of(side, d - 1, core), at).wait_send()
+
+    def settle_early():
+        for k in range(K):
+            die_own(partner, k).wait_recv()
+            die_own(rows, k).wait_send()
+        for side in range(2):
+            raw_sent[side].wait_send()
+            for at in ((0, 0),) + ARRIVALS[side][:SETTLED]:
+                settle(side, at)
+            for at in ARRIVALS[side]:
+                if at[0] < 2:
+                    sent(side, at)
+        for copy in mx_sent + red_sent + r1 + [swap, share, meet]:
+            copy.wait_send()
+
+        @pl.when(first_core)
+        def _():
+            r1_die.wait_send()
+
+        @pl.when(second_core)
+        def _():
+            for copy in rx + ry + [rd]:
+                copy.wait_send()
+
+    for j in range(STEPS):
         if j in between:
             between[j]()
+        if j == STEPS - 2:
+            settle_early()
         arrive(j)
 
-    for k in range(K):
-        die_own(partner, k).wait_recv()
     for side in range(2):
-        for d, k in ((0, 0),) + ARRIVALS[side]:
-            die(side, origin_of(side, d, 1 - core), (d, k)).wait_recv()
-    for k in range(K):
-        die_own(rows, k).wait_send()
-    for side in range(2):
-        raw_sent[side].wait_send()
-        die(side, origin_of(side, 0, core), (0, 0)).wait_send()
-        for d, k in ARRIVALS[side]:
-            die(side, origin_of(side, d, core), (d, k)).wait_send()
-            ring(side, origin_of(side, d - 1, core), (d, k)).wait_send()
-    for copy in mx_sent + red_sent + r1 + [swap, share]:
-        copy.wait_send()
-
-    @pl.when(first_core)
-    def _():
-        r1_die.wait_send()
-
-    @pl.when(second_core)
-    def _():
-        for copy in rx + ry + [rd]:
-            copy.wait_send()
-
-
-PARTS = 11
+        for at in ARRIVALS[side][SETTLED:]:
+            settle(side, at)
+        for at in ARRIVALS[side]:
+            if at[0] >= 2:
+                sent(side, at)
+
+
+PARTS = 2
 
 
 def write(a, b, c, a_out, b_out, c_out, sems):
@@ -314,7 +344,9 @@
             pltpu.VMEM((E, ROWS, LANES), F32),
             pltpu.VMEM((2, LANES), F32),
             pltpu.VMEM((1, LANES), F32),
-            pltpu.VMEM((NR, BLOCKS, LANES), F32),
+            pltpu.VMEM((Z, BLOCKS, LANES), F32),
+            pltpu.VMEM((BLOCKS, LANES), F32),
+            pltpu.VMEM((2, BLOCKS, LANES), F32),
             pltpu.VMEM((2, HALF, LANES), F32),
             pltpu.VMEM((HALF, LANES), F32),
             pltpu.VMEM((Z, HALF, LANES), F32),
@@ -322,7 +354,7 @@
             pltpu.VMEM((2, RAW, LANES), F32),
             pltpu.VMEM((2, LANES), BF16),
             pltpu.VMEM((X * Y, NR, 2, LANES), BF16),
-            dma((4,)), pltpu.SemaphoreType.REGULAR, dma((NR - 1,)), dma((NR,)),
+            dma((4,)), pltpu.SemaphoreType.REGULAR, dma((Z,)), dma((Z + 1,)), dma(()), dma(()),
             dma(()), dma(()), dma((Z - 1,)), dma((Z,)), dma(()), dma(()),
             dma((2,)), dma((2,)), dma((2, 4 * K)), dma((4 * K,)), dma((4 * K,)),
             dma((2, 4 * K)), dma((2, 4 * K)), dma((K,)), dma((K,)),

time: 81.4 us -> 80.8 us (level)
  no operation moved by 1% of the time
where the time goes in v4:
time: 80.8 us; the launch traced here: 80.7 us
  Pallas kernels  80.1 us (99%)
    pallas_call x1, Pallas kernels, on_device(): pl.pallas_call(kernel, name='serve', out_shape=shapes, in_specs=[pl.Block...  75.7 us
    pallas_call x1, Pallas kernels, on_device(): pl.pallas_call(write, name='write', out_shape=shapes, in_specs=[pl.BlockS...  4.4 us

profile of v4, /device:TPU:1, one launch (start us, length us, event | category | flops | bytes accessed | tf_op | source)
XLA Modules:
  0.0 80.7 jit_solution(11594388394319949608)
XLA Ops:
  0.6 75.7 %serve.1 = (bf16[2,1408,2048]{2,1,0:T(8,128)(2,1)S(1)}, f32[2,1408]{1,0:T(2,128)S(1)}, bf16[64,2048]{1,0:T(8,128)(2,1)S(1)}) custom-call(f32[2,1408,128]{2,1,0:T(8,128)} %w_hbm.1, f32[2,128]{1,0:T(2,128)} %bitcast.3, f32[1,128]{1,0:T(1,128)} %bitcast.4), custom_call_target="tpu_custom_call" | custom-call | tf_op jit(solution)/shard_map/serve/pallas_call | solution.py:337
  76.3 4.4 %write.1 = (bf16[2,1408,2048]{2,1,0:T(8,128)(2,1)}, f32[2,1408]{1,0:T(2,128)}, bf16[64,2048]{1,0:T(8,128)(2,1)}) custom-call(bf16[2,1408,2048]{2,1,0:T(8,128)(2,1)S(1)} %get-tuple-element.9.a, f32[2,1408]{1,0:T(2,128)S(1)} %get-tuple-element.10.b, bf16[64,2048]{1,0:T(8,128)(2,1)S(1)} %get-tuple-element.11.c), custom_call_target="tpu_custom_call" | custom-call | tf_op jit(solution)/shard_map/write/pallas_call | solution.py:367

commit v5 on v4

--- a/solution.py
+++ b/solution.py
@@ -17,7 +17,7 @@
 X, Y = 4, 8
 BLOCKS = ROWS // LANES
 HALF = 6
-CHUNKS = ((0, 0, 3), (0, 3, 8), (1, 0, 8), (1, 8, 3))
+CHUNKS = ((0, 0, 3), (0, 3, 8), (1, 0, 6), (1, 6, 5))
 K = len(CHUNKS)
 RAW = CHUNKS[0][2] * LANES
 NEAR = ((0, 1), (1, 0), (0, 2), (0, 3), (1, 1), (2, 0), (1, 2), (1, 3), (2, 1), (2, 2), (2, 3))

time: 80.8 us -> 80.9 us (level)
  no operation moved by 1% of the time
where the time goes in v5:
time: 80.9 us; the launch traced here: 80.8 us
  Pallas kernels  80.1 us (99%)
    pallas_call x1, Pallas kernels, on_device(): pl.pallas_call(kernel, name='serve', out_shape=shapes, in_specs=[pl.Block...  75.7 us
    pallas_call x1, Pallas kernels, on_device(): pl.pallas_call(write, name='write', out_shape=shapes, in_specs=[pl.BlockS...  4.4 us

profile of v5, /device:TPU:1, one launch (start us, length us, event | category | flops | bytes accessed | tf_op | source)
XLA Modules:
  0.0 80.8 jit_solution(11453194794182037113)
XLA Ops:
  0.6 75.7 %serve.1 = (bf16[2,1408,2048]{2,1,0:T(8,128)(2,1)S(1)}, f32[2,1408]{1,0:T(2,128)S(1)}, bf16[64,2048]{1,0:T(8,128)(2,1)S(1)}) custom-call(f32[2,1408,128]{2,1,0:T(8,128)} %w_hbm.1, f32[2,128]{1,0:T(2,128)} %bitcast.3, f32[1,128]{1,0:T(1,128)} %bitcast.4), custom_call_target="tpu_custom_call" | custom-call | tf_op jit(solution)/shard_map/serve/pallas_call | solution.py:337
  76.4 4.4 %write.1 = (bf16[2,1408,2048]{2,1,0:T(8,128)(2,1)}, f32[2,1408]{1,0:T(2,128)}, bf16[64,2048]{1,0:T(8,128)(2,1)}) custom-call(bf16[2,1408,2048]{2,1,0:T(8,128)(2,1)S(1)} %get-tuple-element.9.a, f32[2,1408]{1,0:T(2,128)S(1)} %get-tuple-element.10.b, bf16[64,2048]{1,0:T(8,128)(2,1)S(1)} %get-tuple-element.11.c), custom_call_target="tpu_custom_call" | custom-call | tf_op jit(solution)/shard_map/write/pallas_call | solution.py:367
